TPU v7x, 32 devices: a whole 2x2x4 slice. The times are simulated.
32 devices in a mesh: layer: 2 (over x), blk: 16 (over z, y, core).
Axes of the slice: x: 2, y: 2, z: 4, core: 2. Of those that a mesh axis runs over, the one named last changes fastest.
Arguments:
- sources: bfloat16 [2, 2, 16384, 128], P('layer', None, 'blk'), may hold values from -6 to 6
- near_blocks: bfloat16 [2, 16384, 1024], P('layer', 'blk'), may hold values from -0.09375 to 0.09375
- left_factors: bfloat16 [2, 16384, 512], P('layer', 'blk'), may hold values from -0.125 to 0.125
- right_factors: bfloat16 [2, 16384, 512], P('layer', 'blk'), may hold values from -0.046875 to 0.046875
Outputs:
- traces: bfloat16 [2, 2, 16384, 128], P('layer', None, 'blk')
All inputs are finite; a program needn't handle non-finite values.
Results may differ from a plain program's by a relative error of at most 0.014.
Values may be sent and summed in bfloat16 or wider, within the bound.
A program may use at most 64 MiB of HBM per device.

v0:
```python
import jax
import jax.numpy as jnp
from jax import lax
from jax.sharding import PartitionSpec as P


def passed_along(value, axis, steps):
    count = lax.axis_size(axis)
    leading, last = (max(0, -steps), min(count, count - steps))
    return lax.ppermute(value, axis, [(source, source + steps) for source in range(leading, last)])


def on_device(sources, near_blocks, left_factors, right_factors):
    near_block = near_blocks[0]
    far_left = left_factors[0]
    far_right = right_factors[0]
    own_sources = sources[0]
    layer_count = lax.axis_size("layer")
    position = lax.axis_index("layer")

    def sweep(step, carry):
        arrived, stored = carry
        incoming = (own_sources.astype(jnp.float32) + arrived.astype(jnp.float32)).astype(
            jnp.bfloat16
        )
        near = jnp.einsum("pq,nqb->npb", near_block, incoming, preferred_element_type=jnp.float32)
        partial_value = jnp.einsum(
            "pr,npb->nrb", far_right, incoming, preferred_element_type=jnp.float32
        )
        coeff = lax.psum(partial_value, "blk").astype(jnp.bfloat16)
        result = (
            near + jnp.einsum("pr,nrb->npb", far_left, coeff, preferred_element_type=jnp.float32)
        ).astype(jnp.bfloat16)
        stored = jnp.where(step == position, result, stored)
        arrived = passed_along(result, "layer", 1)
        return (arrived, stored)

    start = (jnp.zeros(own_sources.shape, jnp.bfloat16), jnp.zeros(own_sources.shape, jnp.bfloat16))
    final = lax.fori_loop(0, layer_count, sweep, start)
    stored = final[1]
    return stored[None]


def solution(mesh):
    return jax.shard_map(
        on_device,
        mesh=mesh,
        in_specs=(
            P("layer", None, "blk", None),
            P("layer", "blk", None),
            P("layer", "blk", None),
            P("layer", "blk", None),
        ),
        out_specs=P("layer", None, "blk", None),
        check_vma=False,
    )
```

profile of v0, /device:TPU:31, one launch (start us, length us, event | category | flops | bytes accessed | tf_op | source)
XLA Modules:
  0.0 168.8 jit_solution(4320310217462901490)
XLA Ops:
  0.0 1.2 copy.5
  1.3 0.1 broadcast.3
  1.3 166.4 %while.16 = (s32[]{:T(128)}, bf16[2,1024,128]{1,2,0:T(8,128)(2,1)S(1)}, bf16[2,1024,128]{1,2,0:T(8,128)(2,1)S(1)}, bf16[2,1024,128]{1,2,0:T(8,128)(2,1)S(1)}, bf...) while((s32[]{:T(128)}, ...), condition=%wide.region_2.3_spmd.clone, body=%wide.region_0.2_spmd.clone.sunk | while | flops 1077018624 | bytes 17825980 | solution.py:39
  1.3 1.7 convolution_bitcast_fusion.2
  3.0 62.9 %all-reduce.1 = bf16[2,512,128]{1,2,0:T(8,128)(2,1)S(1)} all-reduce(f32[2,512,128]{1,2,0:T(8,128)S(1)} %convolution_bitcast_fusion.2), channel_id=1, replica_groups=mesh['layer'=2,'blk'=16] {'blk'}, use_global_device_ids=true, to_apply=%region_1.0 | all-reduce | flops 131072 | bytes 786432 | tf_op jit(solution)/shard_map/while/body/eval_jaxpr/psum | solution.py:30
  65.9 0.0 copy-start
  65.9 2.4 %fusion.15 = f32[2,128,1024]{2,1,0:T(8,128)S(1)} fusion(bf16[1024,1024]{1,0:T(8,128)(2,1)} %get-tuple-element.267, bf16[2,1024,128]{1,2,0:T(8,128)(2,1)S(1)} %get-tuple-element.254, bf16[2,1024,128]{1,2,0:T(8,128)(2,1)S(1)} %get-tuple-element.266), kind=kOutput, calls=%fused_computation.clone.1 | convolution fusion | flops 537919488 | bytes 4194304 | tf_op jit(solution)/shard_map/while/body/eval_jaxpr/pq,nqb->npb/dot_general | solution.py:26
  68.3 0.0 copy-done
  68.3 0.6 select_select_fusion.2
  68.9 1.3 collective-permute-start
  70.2 14.3 %collective-permute-done = bf16[2,1024,128]{1,2,0:T(8,128)(2,1)S(1)} collective-permute-done((bf16[2,1024,128]{1,2,0:T(8,128)(2,1)S(1)}, bf16[2,1024,128]{1,2,0:T(8,128)(2,1)S(1)}, u32[]{:S(2)}, u32[]{:S(2)}) %collective-permute-start) | collective-permute-done | bytes 524320 | tf_op jit(solution)/shard_map/while/body/eval_jaxpr/ppermute | solution.py:10
  84.5 1.7 convolution_bitcast_fusion.2
  86.2 62.9 %all-reduce.1 = bf16[2,512,128]{1,2,0:T(8,128)(2,1)S(1)} all-reduce(f32[2,512,128]{1,2,0:T(8,128)S(1)} %convolution_bitcast_fusion.2), channel_id=1, replica_groups=mesh['layer'=2,'blk'=16] {'blk'}, use_global_device_ids=true, to_apply=%region_1.0 | all-reduce | flops 131072 | bytes 786432 | tf_op jit(solution)/shard_map/while/body/eval_jaxpr/psum | solution.py:30
  149.1 0.0 copy-start
  149.1 2.4 %fusion.15 = f32[2,128,1024]{2,1,0:T(8,128)S(1)} fusion(bf16[1024,1024]{1,0:T(8,128)(2,1)} %get-tuple-element.267, bf16[2,1024,128]{1,2,0:T(8,128)(2,1)S(1)} %get-tuple-element.254, bf16[2,1024,128]{1,2,0:T(8,128)(2,1)S(1)} %get-tuple-element.266), kind=kOutput, calls=%fused_computation.clone.1 | convolution fusion | flops 537919488 | bytes 4194304 | tf_op jit(solution)/shard_map/while/body/eval_jaxpr/pq,nqb->npb/dot_general | solution.py:26
  151.5 0.0 copy-done
  151.5 0.6 select_select_fusion.2
  152.1 1.3 collective-permute-start
  153.4 14.3 %collective-permute-done = bf16[2,1024,128]{1,2,0:T(8,128)(2,1)S(1)} collective-permute-done((bf16[2,1024,128]{1,2,0:T(8,128)(2,1)S(1)}, bf16[2,1024,128]{1,2,0:T(8,128)(2,1)S(1)}, u32[]{:S(2)}, u32[]{:S(2)}) %collective-permute-start) | collective-permute-done | bytes 524320 | tf_op jit(solution)/shard_map/while/body/eval_jaxpr/ppermute | solution.py:10
  167.8 1.0 copy.6
  (1 shorter events, 0.0 us)
Async XLA Ops:
  65.9 2.4 %copy-start = (bf16[1024,512]{1,0:T(8,128)(2,1)S(1)}, bf16[1024,512]{1,0:T(8,128)(2,1)}, u32[]{:S(2)}) copy-start(bf16[1024,512]{1,0:T(8,128)(2,1)} %get-tuple-element.269) | copy-start | bytes 3145732 | tf_op jit(solution)/shard_map/while
  68.9 15.6 %collective-permute-start = (bf16[2,1024,128]{1,2,0:T(8,128)(2,1)S(1)}, bf16[2,1024,128]{1,2,0:T(8,128)(2,1)S(1)}, u32[]{:S(2)}, u32[]{:S(2)}) collective-permute-start(bf16[2,1024,128]{1,2,0:T(8,128)(2,1)S(1)} %get-tuple-element.241), channel_id=1, source_target_pairs={{0,16},{1,17},{2,18},{3,19},{4,20},{5,21},{6,22},{7,23},{8,24},{9,... | collective-permute-start | bytes 1572872 | tf_op jit(solution)/shard_map/while/body/eval_jaxpr/ppermute | solution.py:10
  149.1 2.5 %copy-start = (bf16[1024,512]{1,0:T(8,128)(2,1)S(1)}, bf16[1024,512]{1,0:T(8,128)(2,1)}, u32[]{:S(2)}) copy-start(bf16[1024,512]{1,0:T(8,128)(2,1)} %get-tuple-element.269) | copy-start | bytes 3145732 | tf_op jit(solution)/shard_map/while
  152.1 15.6 %collective-permute-start = (bf16[2,1024,128]{1,2,0:T(8,128)(2,1)S(1)}, bf16[2,1024,128]{1,2,0:T(8,128)(2,1)S(1)}, u32[]{:S(2)}, u32[]{:S(2)}) collective-permute-start(bf16[2,1024,128]{1,2,0:T(8,128)(2,1)S(1)} %get-tuple-element.241), channel_id=1, source_target_pairs={{0,16},{1,17},{2,18},{3,19},{4,20},{5,21},{6,22},{7,23},{8,24},{9,... | collective-permute-start | bytes 1572872 | tf_op jit(solution)/shard_map/while/body/eval_jaxpr/ppermute | solution.py:10
where the time goes:
time: 169 us
  blocking collectives  126 us (75%)
  waiting for transfers between devices  28.6 us (17%)
  matrix products  9.35 us (6%)
  starting transfers between devices  2.58 us (2%)
  local copies, waits for them, and re-layouts  2.31 us (1%)
    psum x2, blocking collectives, sweep(): coeff = lax.psum(partial_value, 'blk').astype(jnp.bfloat16)  126 us
    ppermute x2, waiting for transfers between devices, passed_along(): lax.ppermute(value, axis, [(source, source + steps) for source in range(l...  28.6 us
    dot_general x2, matrix products, sweep(): jnp.einsum('pq,nqb->npb', near_block, incoming, preferred_element_type=jn...  4.85 us
  transfers between devices with their start and end apart: 2, of which 2 were waited for; matrix products, arithmetic and copies ran while one was open for 0% of the time, Pallas kernels for 0%

commit v1 on v0

v1 whole, which is shorter than its diff:
```python
import functools

import jax
import jax.numpy as jnp
from jax import lax
from jax.experimental import pallas as pl
from jax.experimental.pallas import tpu as pltpu
from jax.sharding import PartitionSpec as P

MESH = pl.DeviceIdType.MESH
F32 = jnp.float32
BF16 = jnp.bfloat16


def sweep_kernel(
    layers, blocks, pieces, x_parts,
    src_hbm, near_hbm, left_hbm, right_hbm, out_hbm,
    src, near_w, left_w, right_w, inc, arrived, part, core_in, chip_sum,
    scatter_in, coeff, near, result,
    load_sem, core_send, core_recv, rs_send, rs_recv, ag_send, ag_recv,
    fw_send, fw_recv, x_send, x_recv, out_sem,
):
    layer = lax.axis_index("layer")
    blk = lax.axis_index("blk")
    chips = blocks // 2
    chip, core = blk // 2, lax.rem(blk, 2)
    batches, points, srcs = src.shape
    rank = left_w.shape[1]
    half = rank // 2
    rows = half // pieces
    sub = points // x_parts
    partner = (layer, chip * 2 + (1 - core))

    loads = [
        pltpu.make_async_copy(right_hbm.at[0], right_w, load_sem.at[0]),
        pltpu.make_async_copy(src_hbm.at[0], src, load_sem.at[1]),
        pltpu.make_async_copy(near_hbm.at[0], near_w, load_sem.at[2]),
        pltpu.make_async_copy(left_hbm.at[0], left_w, load_sem.at[3]),
    ]
    for load in loads:
        load.start()

    def peer(i):
        return lax.rem(chip + i, chips)

    barrier = pltpu.get_barrier_semaphore()

    def greet(i, carry):
        pl.semaphore_signal(barrier, inc=1, device_id=(layer, peer(i) * 2 + core), device_id_type=MESH)
        return carry

    lax.fori_loop(1, chips, greet, 0)
    pl.semaphore_signal(barrier, inc=1, device_id=partner, device_id_type=MESH)

    @pl.when(layer > 0)
    def _():
        pl.semaphore_signal(barrier, inc=1, device_id=(layer - 1, blk), device_id_type=MESH)

    @pl.when(layer < layers - 1)
    def _():
        pl.semaphore_signal(barrier, inc=1, device_id=(layer + 1, blk), device_id_type=MESH)

    before = lax.div(layer + layers - 1, layers)
    after = lax.div(2 * layers - 2 - layer, layers)
    pl.semaphore_wait(barrier, chips + before + after)

    def core_copy(b):
        return pltpu.make_async_remote_copy(
            src_ref=part.at[b, pl.ds(pl.multiple_of((1 - core) * half, half), half)],
            dst_ref=core_in.at[b],
            send_sem=core_send.at[b], recv_sem=core_recv.at[b],
            device_id=partner, device_id_type=MESH,
        )

    def rs_copy(b, j):
        return pltpu.make_async_remote_copy(
            src_ref=chip_sum.at[b, pl.ds(pl.multiple_of(j * rows, rows), rows)],
            dst_ref=scatter_in.at[b, chip],
            send_sem=rs_send.at[b, j], recv_sem=rs_recv.at[b, chip],
            device_id=(layer, j * 2 + core), device_id_type=MESH,
        )

    def rs_arrival(b, j):
        return pltpu.make_async_remote_copy(
            src_ref=scatter_in.at[b, j], dst_ref=scatter_in.at[b, j],
            send_sem=rs_send.at[b, j], recv_sem=rs_recv.at[b, j],
            device_id=partner, device_id_type=MESH,
        )

    def piece(b, side, j):
        return coeff.at[b, pl.ds(pl.multiple_of(side * half + j * rows, rows), rows)]

    def ag_copy(b, j):
        return pltpu.make_async_remote_copy(
            src_ref=piece(b, core, chip), dst_ref=piece(b, core, chip),
            send_sem=ag_send.at[b, j], recv_sem=ag_recv.at[b, chip],
            device_id=(layer, j * 2 + core), device_id_type=MESH,
        )

    def ag_arrival(b, j):
        return pltpu.make_async_remote_copy(
            src_ref=piece(b, core, j), dst_ref=piece(b, core, j),
            send_sem=ag_send.at[b, j], recv_sem=ag_recv.at[b, j],
            device_id=partner, device_id_type=MESH,
        )

    def fw_copy(b, j):
        return pltpu.make_async_remote_copy(
            src_ref=piece(b, core, j), dst_ref=piece(b, core, j),
            send_sem=fw_send.at[b, j], recv_sem=fw_recv.at[b, j],
            device_id=partner, device_id_type=MESH,
        )

    def fw_arrival(b, j):
        return pltpu.make_async_remote_copy(
            src_ref=piece(b, 1 - core, j), dst_ref=piece(b, 1 - core, j),
            send_sem=fw_send.at[b, j], recv_sem=fw_recv.at[b, j],
            device_id=partner, device_id_type=MESH,
        )

    def x_copy(b, k):
        return pltpu.make_async_remote_copy(
            src_ref=result.at[b, pl.ds(k * sub, sub)],
            dst_ref=arrived.at[b, pl.ds(k * sub, sub)],
            send_sem=x_send.at[b, k], recv_sem=x_recv.at[b, k],
            device_id=(lax.rem(layer + 1, layers), blk), device_id_type=MESH,
        )

    def out_copy(b):
        return pltpu.make_async_copy(result.at[b], out_hbm.at[0, b], out_sem.at[b])

    owns = chip < pieces

    def each_peer(action, only_owners=False):
        def body(i, carry):
            j = peer(i)
            if only_owners and pieces < chips:
                @pl.when(j < pieces)
                def _():
                    action(j)
            else:
                action(j)
            return carry

        lax.fori_loop(1, chips, body, 0)

    def take_in(b, first):
        if first:
            inc[b] = src[b]
        else:
            for k in range(x_parts):
                x_copy(b, k).wait_recv()
            inc[b] = (src[b].astype(F32) + arrived[b].astype(F32)).astype(BF16)

    def partial_sum(b):
        part[b] = lax.dot_general(
            right_w[...], inc[b], (((0,), (0,)), ((), ())), preferred_element_type=F32
        ).astype(BF16)
        core_copy(b).start()

    def scatter(b):
        core_copy(b).wait_recv()
        mine = part[b, pl.ds(pl.multiple_of(core * half, half), half)]
        chip_sum[b] = (mine.astype(F32) + core_in[b].astype(F32)).astype(BF16)
        each_peer(lambda j: rs_copy(b, j).start(), True)

    def near_product(b):
        near[b] = jnp.dot(near_w[...], inc[b], preferred_element_type=F32)

    def gather(b):
        @pl.when(owns)
        def _():
            each_peer(lambda j: rs_arrival(b, j).wait_recv())
            scatter_in[b, chip] = chip_sum[b, pl.ds(pl.multiple_of(chip * rows, rows), rows)]
            total = jnp.sum(scatter_in[b].astype(F32), axis=0)
            coeff[b, pl.ds(pl.multiple_of(core * half + chip * rows, rows), rows)] = total.astype(BF16)
            each_peer(lambda j: ag_copy(b, j).start())
            fw_copy(b, chip).start()

    def forward(b):
        def pass_on(j):
            ag_arrival(b, j).wait_recv()
            fw_copy(b, j).start()

        each_peer(pass_on, True)

    def finish(b):
        def body(j, carry):
            fw_arrival(b, j).wait_recv()
            return carry

        lax.fori_loop(0, pieces, body, 0)
        for k in range(x_parts):
            at = pl.ds(k * sub, sub)
            result[b, at] = (
                near[b, at] + jnp.dot(left_w[at], coeff[b], preferred_element_type=F32)
            ).astype(BF16)

            @pl.when(layer < layers - 1)
            def _():
                x_copy(b, k).start()

        out_copy(b).start()

    loads[0].wait()
    loads[1].wait()

    every = range(batches)

    @pl.when(layer == 0)
    def _():
        for b in every:
            take_in(b, True)
            partial_sum(b)
        for b in every:
            scatter(b)
        loads[2].wait()
        for b in every:
            near_product(b)
        for b in every:
            gather(b)
        loads[3].wait()
        for b in every:
            forward(b)
        for b in every:
            finish(b)

    @pl.when(layer > 0)
    def _():
        loads[2].wait()
        loads[3].wait()
        for b in every:
            take_in(b, False)
            partial_sum(b)
            scatter(b)
            if b > 0:
                gather(b - 1)
            near_product(b)
            if b > 0:
                forward(b - 1)
        gather(batches - 1)
        for b in range(batches - 1):
            finish(b)
        forward(batches - 1)
        finish(batches - 1)

    for b in every:
        core_copy(b).wait_send()
        each_peer(lambda j: rs_copy(b, j).wait_send(), True)

        @pl.when(owns)
        def _():
            each_peer(lambda j: ag_copy(b, j).wait_send())

        def body(j, carry):
            fw_copy(b, j).wait_send()
            return carry

        lax.fori_loop(0, pieces, body, 0)

        @pl.when(layer < layers - 1)
        def _():
            for k in range(x_parts):
                x_copy(b, k).wait_send()

        out_copy(b).wait()


def solution(mesh):
    layers, blocks = mesh.shape["layer"], mesh.shape["blk"]

    def on_device(sources, near_blocks, left_factors, right_factors):
        _, batches, points, srcs = sources.shape
        rank = left_factors.shape[2]
        half = rank // 2
        chips = blocks // 2
        pieces = min(chips, half // 16)
        rows = half // pieces
        x_parts = 2
        dma = pltpu.SemaphoreType.DMA
        return pl.pallas_call(
            functools.partial(sweep_kernel, layers, blocks, pieces, x_parts),
            out_shape=jax.ShapeDtypeStruct(sources.shape, BF16),
            in_specs=[pl.BlockSpec(memory_space=pl.ANY)] * 4,
            out_specs=pl.BlockSpec(memory_space=pl.ANY),
            scratch_shapes=[
                pltpu.VMEM((batches, points, srcs), BF16),
                pltpu.VMEM(near_blocks.shape[1:], BF16),
                pltpu.VMEM(left_factors.shape[1:], BF16),
                pltpu.VMEM(right_factors.shape[1:], BF16),
                pltpu.VMEM((batches, points, srcs), BF16),
                pltpu.VMEM((batches, points, srcs), BF16),
                pltpu.VMEM((batches, rank, srcs), BF16),
                pltpu.VMEM((batches, half, srcs), BF16),
                pltpu.VMEM((batches, half, srcs), BF16),
                pltpu.VMEM((batches, chips, rows, srcs), BF16),
                pltpu.VMEM((batches, rank, srcs), BF16),
                pltpu.VMEM((batches, points, srcs), F32),
                pltpu.VMEM((batches, points, srcs), BF16),
                dma((4,)),
                dma((batches,)), dma((batches,)),
                dma((batches, chips)), dma((batches, chips)),
                dma((batches, chips)), dma((batches, chips)),
                dma((batches, pieces)), dma((batches, pieces)),
                dma((batches, x_parts)), dma((batches, x_parts)),
                dma((batches,)),
            ],
            compiler_params=pltpu.CompilerParams(collective_id=0, has_side_effects=True),
        )(sources, near_blocks, left_factors, right_factors)

    return jax.shard_map(
        on_device,
        mesh=mesh,
        in_specs=(
            P("layer", None, "blk", None),
            P("layer", "blk", None),
            P("layer", "blk", None),
            P("layer", "blk", None),
        ),
        out_specs=P("layer", None, "blk", None),
        check_vma=False,
    )
```

time: 169 us -> 46.8 us (0.28)
  the two profiles are of different devices: /device:TPU:31 before, /device:TPU:3 now
where the time goes in v1:
time: 46.8 us; the launch traced here: 46.6 us
  Pallas kernels  44.7 us (96%)
  local copies, waits for them, and re-layouts  1.87 us (4%)
    pallas_call x1, Pallas kernels, on_device(): pl.pallas_call(functools.partial(sweep_kernel, layers, blocks, pieces, x_...  44.7 us
    unnamed x1, local copies, waits for them, and re-layouts  1.87 us

profile of v1, /device:TPU:3, one launch (start us, length us, event | category | flops | bytes accessed | tf_op | source)
XLA Modules:
  0.0 46.6 jit_solution(1503112773411637917)
XLA Ops:
  0.0 44.7 %shard_map.46 = bf16[1,2,1024,128]{3,2,1,0:T(8,128)(2,1)} custom-call(bf16[1,2,1024,128]{3,2,1,0:T(8,128)(2,1)} %src_hbm.1, bf16[1,1024,1024]{2,1,0:T(8,128)(2,1)} %near_hbm.1, bf16[1,1024,512]{2,1,0:T(8,128)(2,1)} %left_hbm.1, bf16[1,1024,512]{2,1,0:T(8,128)(2,1)} %right_hbm.1), custom_call_target="tpu_custom_call" | custom-call | tf_op jit(solution)/shard_map/pallas_call | solution.py:281
  44.8 1.9 %copy.6 = bf16[1,2,1024,128]{3,2,1,0:T(8,128)(2,1)} copy(bf16[1,2,1024,128]{3,2,1,0:T(8,128)(2,1)} %shard_map.46) | data formatting | bytes 1048576

commit v2 on v0

v2 whole, which is shorter than its diff:
```python
import functools

import jax
import jax.numpy as jnp
from jax import lax
from jax.experimental import pallas as pl
from jax.experimental.pallas import tpu as pltpu
from jax.sharding import PartitionSpec as P

MESH = pl.DeviceIdType.MESH
F32 = jnp.float32
BF16 = jnp.bfloat16


def sweep_kernel(
    layers, blocks, pieces, split,
    src_hbm, near_hbm, left_hbm, right_hbm, out_hbm,
    src, near_w, left_w, right_w, inc, arrived, part, core_in, chip_sum,
    scatter_in, coeff, near, result,
    next_right, last_left, near_out, near_in, carry_out, carry_in,
    load_sem, core_send, core_recv, rs_send, rs_recv, ag_send, ag_recv,
    fw_send, fw_recv, x_send, x_recv, near_send, near_recv, up_send, up_recv,
    carry_send, carry_recv, factor_send, factor_recv, out_sem,
):
    layer = lax.axis_index("layer")
    blk = lax.axis_index("blk")
    chips = blocks // 2
    chip, core = blk // 2, lax.rem(blk, 2)
    batches, points, srcs = src.shape
    rank = left_w.shape[1]
    half = rank // 2
    rows = half // pieces
    every = range(batches)
    columns = [slice(b * srcs, (b + 1) * srcs) for b in every]
    front, back = pl.ds(0, split), pl.ds(split, points - split)
    partner = (layer, chip * 2 + (1 - core))
    above = (lax.rem(layer + 1, layers), blk)
    below = (lax.rem(layer + layers - 1, layers), blk)
    has_next = layer < layers - 1
    has_last = layer > 0

    loads = [
        pltpu.make_async_copy(right_hbm.at[0], right_w, load_sem.at[0]),
        pltpu.make_async_copy(src_hbm.at[0], src, load_sem.at[1]),
        pltpu.make_async_copy(near_hbm.at[0], near_w, load_sem.at[2]),
        pltpu.make_async_copy(left_hbm.at[0], left_w, load_sem.at[3]),
    ]
    for load in loads:
        load.start()

    def peer(i):
        return lax.rem(chip + i, chips)

    barrier = pltpu.get_barrier_semaphore()

    def greet(i, carry):
        pl.semaphore_signal(barrier, inc=1, device_id=(layer, peer(i) * 2 + core), device_id_type=MESH)
        return carry

    lax.fori_loop(1, chips, greet, 0)
    pl.semaphore_signal(barrier, inc=1, device_id=partner, device_id_type=MESH)

    @pl.when(has_last)
    def _():
        pl.semaphore_signal(barrier, inc=1, device_id=below, device_id_type=MESH)

    @pl.when(has_next)
    def _():
        pl.semaphore_signal(barrier, inc=1, device_id=above, device_id_type=MESH)

    before = lax.div(layer + layers - 1, layers)
    after = lax.div(2 * layers - 2 - layer, layers)
    pl.semaphore_wait(barrier, chips + before + after)

    def remote(src_ref, dst_ref, send_sem, recv_sem, device):
        return pltpu.make_async_remote_copy(
            src_ref=src_ref, dst_ref=dst_ref, send_sem=send_sem, recv_sem=recv_sem,
            device_id=device, device_id_type=MESH,
        )

    def core_copy(n):
        return remote(
            part.at[n, pl.ds(pl.multiple_of((1 - core) * half, half), half)], core_in.at[n],
            core_send.at[n], core_recv.at[n], partner,
        )

    def rs_copy(n, j):
        return remote(
            chip_sum.at[n, pl.ds(pl.multiple_of(j * rows, rows), rows)], scatter_in.at[n, chip],
            rs_send.at[n, j], rs_recv.at[n, chip], (layer, j * 2 + core),
        )

    def rs_arrival(n, j):
        return remote(
            scatter_in.at[n, j], scatter_in.at[n, j], rs_send.at[n, j], rs_recv.at[n, j], partner,
        )

    def piece(n, side, j):
        q, b = divmod(n, batches)
        return coeff.at[
            q, pl.ds(pl.multiple_of(side * half + j * rows, rows), rows), pl.ds(b * srcs, srcs)
        ]

    def ag_copy(n, j):
        own = piece(n, core, chip)
        return remote(own, own, ag_send.at[n, j], ag_recv.at[n, chip], (layer, j * 2 + core))

    def ag_arrival(n, j):
        there = piece(n, core, j)
        return remote(there, there, ag_send.at[n, j], ag_recv.at[n, j], partner)

    def fw_copy(n, j):
        there = piece(n, core, j)
        return remote(there, there, fw_send.at[n, j], fw_recv.at[n, j], partner)

    def fw_arrival(n, j):
        there = piece(n, 1 - core, j)
        return remote(there, there, fw_send.at[n, j], fw_recv.at[n, j], partner)

    def up_copy(b):
        return remote(
            piece(b, core, chip), piece(batches + b, core, chip), up_send.at[b], up_recv.at[b], above
        )

    def carry_copy(b):
        return remote(carry_out.at[b], carry_in.at[b], carry_send.at[b], carry_recv.at[b], above)

    def x_copy(b):
        return remote(result.at[b, front], arrived.at[b], x_send.at[b], x_recv.at[b], above)

    def near_copy(b):
        return remote(near_out.at[b], near_in.at[b], near_send.at[b], near_recv.at[b], above)

    left_copy = remote(
        left_hbm.at[0, back], last_left, factor_send.at[0], factor_recv.at[0], above
    )
    right_copy = remote(
        right_hbm.at[0, front], next_right, factor_send.at[1], factor_recv.at[1], below
    )

    def out_copy(b):
        return pltpu.make_async_copy(result.at[b], out_hbm.at[0, b], out_sem.at[b])

    @pl.when(has_next)
    def _():
        left_copy.start()

    @pl.when(has_last)
    def _():
        right_copy.start()

    owns = chip < pieces

    def each_peer(action, only_owners=False):
        def body(i, carry):
            j = peer(i)
            if only_owners and pieces < chips:
                @pl.when(j < pieces)
                def _():
                    action(j)
            else:
                action(j)
            return carry

        lax.fori_loop(1, chips, body, 0)

    def each_piece(action):
        def body(j, carry):
            action(j)
            return carry

        lax.fori_loop(0, pieces, body, 0)

    def over_points(weights, values):
        return lax.dot_general(weights, values, (((0,), (0,)), ((), ())), preferred_element_type=F32)

    def send_partial(q, value):
        for b in every:
            part[q * batches + b] = value[:, columns[b]].astype(BF16)
            core_copy(q * batches + b).start()

    def scatter(n):
        core_copy(n).wait_recv()
        mine = part[n, pl.ds(pl.multiple_of(core * half, half), half)]
        chip_sum[n] = (mine.astype(F32) + core_in[n].astype(F32)).astype(BF16)
        each_peer(lambda j: rs_copy(n, j).start(), True)

    def piece_total(n):
        each_peer(lambda j: rs_arrival(n, j).wait_recv())
        scatter_in[n, chip] = chip_sum[n, pl.ds(pl.multiple_of(chip * rows, rows), rows)]
        return jnp.sum(scatter_in[n].astype(F32), axis=0)

    def gather(b, first):
        @pl.when(owns)
        def _():
            total = piece_total(b)
            if not first:
                carry_copy(b).wait_recv()
                total = total + carry_in[b].astype(F32)
            coeff[
                0, pl.ds(pl.multiple_of(core * half + chip * rows, rows), rows), columns[b]
            ] = total.astype(BF16)
            each_peer(lambda j: ag_copy(b, j).start())
            fw_copy(b, chip).start()

            @pl.when(has_next)
            def _():
                up_copy(b).start()

    def gather_last(b):
        @pl.when(owns)
        def _():
            up_copy(b).wait_recv()
            each_peer(lambda j: ag_copy(batches + b, j).start())
            fw_copy(batches + b, chip).start()

    def forward(n):
        def pass_on(j):
            ag_arrival(n, j).wait_recv()
            fw_copy(n, j).start()

        each_peer(pass_on, True)

    def near_product(at):
        near[at] = jnp.dot(near_w[at], inc[...], preferred_element_type=F32)

    def send_near():
        @pl.when(has_next)
        def _():
            for b in every:
                near_out[b] = near[back, columns[b]].astype(BF16)
                near_copy(b).start()

    def finish():
        for b in every:
            each_piece(lambda j: fw_arrival(b, j).wait_recv())
        for at in (front, back):
            value = (
                near[at] + jnp.dot(left_w[at], coeff[0], preferred_element_type=F32)
            ).astype(BF16)
            for b in every:
                result[b, at] = value[:, columns[b]]
            if at is front:
                @pl.when(has_next)
                def _():
                    right_copy.wait_recv()
                    send_partial(1, over_points(next_right[...], value))
                    for b in every:
                        x_copy(b).start()
        for b in every:
            out_copy(b).start()

        @pl.when(has_next)
        def _():
            for b in every:
                scatter(batches + b)
            for b in every:
                @pl.when(owns)
                def _():
                    carry_out[b] = piece_total(batches + b).astype(BF16)
                    carry_copy(b).start()

    loads[0].wait()
    loads[1].wait()

    @pl.when(layer == 0)
    def _():
        for b in every:
            inc[:, columns[b]] = src[b]
        send_partial(0, over_points(right_w[...], inc[...]))
        loads[2].wait()
        near_product(back)
        send_near()
        for b in every:
            scatter(b)
        near_product(front)
        for b in every:
            gather(b, True)
        loads[3].wait()
        for b in every:
            forward(b)
        finish()

    @pl.when(has_last)
    def _():
        for b in every:
            inc[front, columns[b]] = src[b, front]
        base = over_points(right_w[front], inc[front])
        loads[2].wait()
        loads[3].wait()
        left_copy.wait_recv()
        for b in every:
            near_copy(b).wait_recv()
        for b in every:
            gather_last(b)
        for b in every:
            forward(batches + b)
        for b in every:
            each_piece(lambda j: fw_arrival(batches + b, j).wait_recv())
        far = jnp.dot(last_left[...], coeff[1], preferred_element_type=F32)
        for b in every:
            trace = (near_in[b].astype(F32) + far[:, columns[b]]).astype(BF16)
            inc[back, columns[b]] = (src[b, back].astype(F32) + trace.astype(F32)).astype(BF16)
        send_partial(0, base + over_points(right_w[back], inc[back]))
        for b in every:
            scatter(b)
        for b in every:
            x_copy(b).wait_recv()
            inc[front, columns[b]] = (
                src[b, front].astype(F32) + arrived[b].astype(F32)
            ).astype(BF16)
        near_product(back)
        send_near()
        near_product(front)
        for b in every:
            gather(b, False)
        for b in every:
            forward(b)
        finish()

    def sent(n):
        core_copy(n).wait_send()
        each_peer(lambda j: rs_copy(n, j).wait_send(), True)

    def gathered(n):
        @pl.when(owns)
        def _():
            each_peer(lambda j: ag_copy(n, j).wait_send())

        each_piece(lambda j: fw_copy(n, j).wait_send())

    for b in every:
        sent(b)
        gathered(b)

        @pl.when(has_last)
        def _():
            gathered(batches + b)

        @pl.when(has_next)
        def _():
            sent(batches + b)
            near_copy(b).wait_send()
            x_copy(b).wait_send()

            @pl.when(owns)
            def _():
                up_copy(b).wait_send()
                carry_copy(b).wait_send()

        out_copy(b).wait()

    @pl.when(has_next)
    def _():
        left_copy.wait_send()

    @pl.when(has_last)
    def _():
        right_copy.wait_send()


def solution(mesh):
    layers, blocks = mesh.shape["layer"], mesh.shape["blk"]

    def on_device(sources, near_blocks, left_factors, right_factors):
        _, batches, points, srcs = sources.shape
        rank = left_factors.shape[2]
        half = rank // 2
        chips = blocks // 2
        pieces = min(chips, half // 16)
        rows = half // pieces
        split = points * 5 // 8
        rest = points - split
        dma = pltpu.SemaphoreType.DMA
        vmem = pltpu.VMEM
        return pl.pallas_call(
            functools.partial(sweep_kernel, layers, blocks, pieces, split),
            out_shape=jax.ShapeDtypeStruct(sources.shape, BF16),
            in_specs=[pl.BlockSpec(memory_space=pl.ANY)] * 4,
            out_specs=pl.BlockSpec(memory_space=pl.ANY),
            scratch_shapes=[
                vmem((batches, points, srcs), BF16),
                vmem(near_blocks.shape[1:], BF16),
                vmem(left_factors.shape[1:], BF16),
                vmem(right_factors.shape[1:], BF16),
                vmem((points, batches * srcs), BF16),
                vmem((batches, split, srcs), BF16),
                vmem((2 * batches, rank, srcs), BF16),
                vmem((2 * batches, half, srcs), BF16),
                vmem((2 * batches, half, srcs), BF16),
                vmem((2 * batches, chips, rows, srcs), BF16),
                vmem((2, rank, batches * srcs), BF16),
                vmem((points, batches * srcs), F32),
                vmem((batches, points, srcs), BF16),
                vmem((split, rank), BF16),
                vmem((rest, rank), BF16),
                vmem((batches, rest, srcs), BF16),
                vmem((batches, rest, srcs), BF16),
                vmem((batches, rows, srcs), BF16),
                vmem((batches, rows, srcs), BF16),
                dma((4,)),
                dma((2 * batches,)), dma((2 * batches,)),
                dma((2 * batches, chips)), dma((2 * batches, chips)),
                dma((2 * batches, chips)), dma((2 * batches, chips)),
                dma((2 * batches, pieces)), dma((2 * batches, pieces)),
                dma((batches,)), dma((batches,)),
                dma((batches,)), dma((batches,)),
                dma((batches,)), dma((batches,)),
                dma((batches,)), dma((batches,)),
                dma((2,)), dma((2,)),
                dma((batches,)),
            ],
            compiler_params=pltpu.CompilerParams(collective_id=0, has_side_effects=True),
        )(sources, near_blocks, left_factors, right_factors)

    return jax.shard_map(
        on_device,
        mesh=mesh,
        in_specs=(
            P("layer", None, "blk", None),
            P("layer", "blk", None),
            P("layer", "blk", None),
            P("layer", "blk", None),
        ),
        out_specs=P("layer", None, "blk", None),
        check_vma=False,
    )
```

time: 169 us -> 41.5 us (0.25)
  the two profiles are of different devices: /device:TPU:31 before, /device:TPU:3 now
where the time goes in v2:
time: 41.5 us; the launch traced here: 41.3 us
  Pallas kernels  39.5 us (95%)
  local copies, waits for them, and re-layouts  1.87 us (5%)
    pallas_call x1, Pallas kernels, on_device(): pl.pallas_call(functools.partial(sweep_kernel, layers, blocks, pieces, sp...  39.5 us
    unnamed x1, local copies, waits for them, and re-layouts  1.87 us

profile of v2, /device:TPU:3, one launch (start us, length us, event | category | flops | bytes accessed | tf_op | source)
XLA Modules:
  0.0 41.3 jit_solution(12974367187005928156)
XLA Ops:
  0.0 39.5 %shard_map.46 = bf16[1,2,1024,128]{3,2,1,0:T(8,128)(2,1)} custom-call(bf16[1,2,1024,128]{3,2,1,0:T(8,128)(2,1)} %src_hbm.1, bf16[1,1024,1024]{2,1,0:T(8,128)(2,1)} %near_hbm.1, bf16[1,1024,512]{2,1,0:T(8,128)(2,1)} %left_hbm.1, bf16[1,1024,512]{2,1,0:T(8,128)(2,1)} %right_hbm.1), custom_call_target="tpu_custom_call" | custom-call | tf_op jit(solution)/shard_map/pallas_call | solution.py:376
  39.5 1.9 %copy.6 = bf16[1,2,1024,128]{3,2,1,0:T(8,128)(2,1)} copy(bf16[1,2,1024,128]{3,2,1,0:T(8,128)(2,1)} %shard_map.46) | data formatting | bytes 1048576

commit v3 on v2

--- a/solution.py
+++ b/solution.py
@@ -17,7 +17,7 @@
     src_hbm, near_hbm, left_hbm, right_hbm, out_hbm,
     src, near_w, left_w, right_w, inc, arrived, part, core_in, chip_sum,
     scatter_in, coeff, near, result,
-    next_right, last_left, near_out, near_in, carry_out, carry_in,
+    next_right, last_left, near_out, near_in, carry_out, carry_in, base,
     load_sem, core_send, core_recv, rs_send, rs_recv, ag_send, ag_recv,
     fw_send, fw_recv, x_send, x_recv, near_send, near_recv, up_send, up_recv,
     carry_send, carry_recv, factor_send, factor_recv, out_sem,
@@ -70,6 +70,25 @@
 
     before = lax.div(layer + layers - 1, layers)
     after = lax.div(2 * layers - 2 - layer, layers)
+
+    def over_points(weights, values):
+        return lax.dot_general(weights, values, (((0,), (0,)), ((), ())), preferred_element_type=F32)
+
+    loads[0].wait()
+    loads[1].wait()
+
+    @pl.when(layer == 0)
+    def _():
+        for b in every:
+            inc[:, columns[b]] = src[b]
+        base[...] = over_points(right_w[...], inc[...])
+
+    @pl.when(has_last)
+    def _():
+        for b in every:
+            inc[front, columns[b]] = src[b, front]
+        base[...] = over_points(right_w[front], inc[front])
+
     pl.semaphore_wait(barrier, chips + before + after)
 
     def remote(src_ref, dst_ref, send_sem, recv_sem, device):
@@ -131,11 +150,17 @@
     def near_copy(b):
         return remote(near_out.at[b], near_in.at[b], near_send.at[b], near_recv.at[b], above)
 
-    left_copy = remote(
-        left_hbm.at[0, back], last_left, factor_send.at[0], factor_recv.at[0], above
-    )
+    first_rows = points // 4
+
+    def left_copy(k):
+        at, size = (0, first_rows) if k == 0 else (first_rows, points - split - first_rows)
+        return remote(
+            left_hbm.at[0, pl.ds(split + at, size)], last_left.at[pl.ds(at, size)],
+            factor_send.at[k], factor_recv.at[k], above,
+        )
+
     right_copy = remote(
-        right_hbm.at[0, front], next_right, factor_send.at[1], factor_recv.at[1], below
+        right_hbm.at[0, front], next_right, factor_send.at[2], factor_recv.at[2], below
     )
 
     def out_copy(b):
@@ -143,7 +168,7 @@
 
     @pl.when(has_next)
     def _():
-        left_copy.start()
+        left_copy(0).start()
 
     @pl.when(has_last)
     def _():
@@ -171,9 +196,6 @@
 
         lax.fori_loop(0, pieces, body, 0)
 
-    def over_points(weights, values):
-        return lax.dot_general(weights, values, (((0,), (0,)), ((), ())), preferred_element_type=F32)
-
     def send_partial(q, value):
         for b in every:
             part[q * batches + b] = value[:, columns[b]].astype(BF16)
@@ -227,6 +249,7 @@
     def send_near():
         @pl.when(has_next)
         def _():
+            left_copy(1).start()
             for b in every:
                 near_out[b] = near[back, columns[b]].astype(BF16)
                 near_copy(b).start()
@@ -260,22 +283,17 @@
                     carry_out[b] = piece_total(batches + b).astype(BF16)
                     carry_copy(b).start()
 
-    loads[0].wait()
-    loads[1].wait()
-
     @pl.when(layer == 0)
     def _():
-        for b in every:
-            inc[:, columns[b]] = src[b]
-        send_partial(0, over_points(right_w[...], inc[...]))
+        send_partial(0, base[...])
         loads[2].wait()
         near_product(back)
-        send_near()
         for b in every:
             scatter(b)
         near_product(front)
         for b in every:
             gather(b, True)
+        send_near()
         loads[3].wait()
         for b in every:
             forward(b)
@@ -283,25 +301,23 @@
 
     @pl.when(has_last)
     def _():
-        for b in every:
-            inc[front, columns[b]] = src[b, front]
-        base = over_points(right_w[front], inc[front])
         loads[2].wait()
         loads[3].wait()
-        left_copy.wait_recv()
+        left_copy(0).wait_recv()
+        for b in every:
+            gather_last(b)
+        for b in every:
+            forward(batches + b)
+        left_copy(1).wait_recv()
         for b in every:
             near_copy(b).wait_recv()
-        for b in every:
-            gather_last(b)
-        for b in every:
-            forward(batches + b)
         for b in every:
             each_piece(lambda j: fw_arrival(batches + b, j).wait_recv())
         far = jnp.dot(last_left[...], coeff[1], preferred_element_type=F32)
         for b in every:
             trace = (near_in[b].astype(F32) + far[:, columns[b]]).astype(BF16)
             inc[back, columns[b]] = (src[b, back].astype(F32) + trace.astype(F32)).astype(BF16)
-        send_partial(0, base + over_points(right_w[back], inc[back]))
+        send_partial(0, base[...] + over_points(right_w[back], inc[back]))
         for b in every:
             scatter(b)
         for b in every:
@@ -310,10 +326,10 @@
                 src[b, front].astype(F32) + arrived[b].astype(F32)
             ).astype(BF16)
         near_product(back)
+        near_product(front)
+        for b in every:
+            gather(b, False)
         send_near()
-        near_product(front)
-        for b in every:
-            gather(b, False)
         for b in every:
             forward(b)
         finish()
@@ -352,7 +368,8 @@
 
     @pl.when(has_next)
     def _():
-        left_copy.wait_send()
+        left_copy(0).wait_send()
+        left_copy(1).wait_send()
 
     @pl.when(has_last)
     def _():
@@ -369,7 +386,7 @@
         chips = blocks // 2
         pieces = min(chips, half // 16)
         rows = half // pieces
-        split = points * 5 // 8
+        split = points * 19 // 32
         rest = points - split
         dma = pltpu.SemaphoreType.DMA
         vmem = pltpu.VMEM
@@ -398,6 +415,7 @@
                 vmem((batches, rest, srcs), BF16),
                 vmem((batches, rows, srcs), BF16),
                 vmem((batches, rows, srcs), BF16),
+                vmem((rank, batches * srcs), F32),
                 dma((4,)),
                 dma((2 * batches,)), dma((2 * batches,)),
                 dma((2 * batches, chips)), dma((2 * batches, chips)),
@@ -407,7 +425,7 @@
                 dma((batches,)), dma((batches,)),
                 dma((batches,)), dma((batches,)),
                 dma((batches,)), dma((batches,)),
-                dma((2,)), dma((2,)),
+                dma((3,)), dma((3,)),
                 dma((batches,)),
             ],
             compiler_params=pltpu.CompilerParams(collective_id=0, has_side_effects=True),

time: 41.5 us -> 40.4 us (0.973)
  Pallas kernels: 39.5 us -> 38.4 us
    pallas_call x1, Pallas kernels: 39.5 us -> 38.4 us  [on_device(): pl.pallas_call(functools.partial(sweep_kernel, layers, blocks, pieces, sp...]
where the time goes in v3:
time: 40.4 us; the launch traced here: 40.3 us
  Pallas kernels  38.4 us (95%)
  local copies, waits for them, and re-layouts  1.87 us (5%)
    pallas_call x1, Pallas kernels, on_device(): pl.pallas_call(functools.partial(sweep_kernel, layers, blocks, pieces, sp...  38.4 us
    unnamed x1, local copies, waits for them, and re-layouts  1.87 us

profile of v3, /device:TPU:3, one launch (start us, length us, event | category | flops | bytes accessed | tf_op | source)
XLA Modules:
  0.0 40.3 jit_solution(5040399848890925635)
XLA Ops:
  0.0 38.4 %shard_map.46 = bf16[1,2,1024,128]{3,2,1,0:T(8,128)(2,1)} custom-call(bf16[1,2,1024,128]{3,2,1,0:T(8,128)(2,1)} %src_hbm.1, bf16[1,1024,1024]{2,1,0:T(8,128)(2,1)} %near_hbm.1, bf16[1,1024,512]{2,1,0:T(8,128)(2,1)} %left_hbm.1, bf16[1,1024,512]{2,1,0:T(8,128)(2,1)} %right_hbm.1), custom_call_target="tpu_custom_call" | custom-call | tf_op jit(solution)/shard_map/pallas_call | solution.py:393
  38.4 1.9 %copy.6 = bf16[1,2,1024,128]{3,2,1,0:T(8,128)(2,1)} copy(bf16[1,2,1024,128]{3,2,1,0:T(8,128)(2,1)} %shard_map.46) | data formatting | bytes 1048576

commit v4 on v3

--- a/solution.py
+++ b/solution.py
@@ -14,19 +14,20 @@
 
 def sweep_kernel(
     layers, blocks, pieces, split,
-    src_hbm, near_hbm, left_hbm, right_hbm, out_hbm,
+    src_hbm, near_hbm, left_hbm, right_hbm, result_block,
     src, near_w, left_w, right_w, inc, arrived, part, core_in, chip_sum,
-    scatter_in, coeff, near, result,
+    scatter_in, coeff, near,
     next_right, last_left, near_out, near_in, carry_out, carry_in, base,
     load_sem, core_send, core_recv, rs_send, rs_recv, ag_send, ag_recv,
     fw_send, fw_recv, x_send, x_recv, near_send, near_recv, up_send, up_recv,
-    carry_send, carry_recv, factor_send, factor_recv, out_sem,
+    carry_send, carry_recv, factor_send, factor_recv,
 ):
     layer = lax.axis_index("layer")
     blk = lax.axis_index("blk")
     chips = blocks // 2
     chip, core = blk // 2, lax.rem(blk, 2)
     batches, points, srcs = src.shape
+    result = result_block.at[0]
     rank = left_w.shape[1]
     half = rank // 2
     rows = half // pieces
@@ -162,9 +163,6 @@
     right_copy = remote(
         right_hbm.at[0, front], next_right, factor_send.at[2], factor_recv.at[2], below
     )
-
-    def out_copy(b):
-        return pltpu.make_async_copy(result.at[b], out_hbm.at[0, b], out_sem.at[b])
 
     @pl.when(has_next)
     def _():
@@ -270,9 +268,6 @@
                     send_partial(1, over_points(next_right[...], value))
                     for b in every:
                         x_copy(b).start()
-        for b in every:
-            out_copy(b).start()
-
         @pl.when(has_next)
         def _():
             for b in every:
@@ -364,7 +359,6 @@
                 up_copy(b).wait_send()
                 carry_copy(b).wait_send()
 
-        out_copy(b).wait()
 
     @pl.when(has_next)
     def _():
@@ -393,8 +387,8 @@
         return pl.pallas_call(
             functools.partial(sweep_kernel, layers, blocks, pieces, split),
             out_shape=jax.ShapeDtypeStruct(sources.shape, BF16),
-            in_specs=[pl.BlockSpec(memory_space=pl.ANY)] * 4,
-            out_specs=pl.BlockSpec(memory_space=pl.ANY),
+            in_specs=[pl.BlockSpec(memory_space=pltpu.HBM)] * 4,
+            out_specs=pl.BlockSpec(memory_space=pltpu.VMEM),
             scratch_shapes=[
                 vmem((batches, points, srcs), BF16),
                 vmem(near_blocks.shape[1:], BF16),
@@ -408,7 +402,6 @@
                 vmem((2 * batches, chips, rows, srcs), BF16),
                 vmem((2, rank, batches * srcs), BF16),
                 vmem((points, batches * srcs), F32),
-                vmem((batches, points, srcs), BF16),
                 vmem((split, rank), BF16),
                 vmem((rest, rank), BF16),
                 vmem((batches, rest, srcs), BF16),
@@ -426,10 +419,9 @@
                 dma((batches,)), dma((batches,)),
                 dma((batches,)), dma((batches,)),
                 dma((3,)), dma((3,)),
-                dma((batches,)),
             ],
-            compiler_params=pltpu.CompilerParams(collective_id=0, has_side_effects=True),
-        )(sources, near_blocks, left_factors, right_factors)
+            compiler_params=pltpu.CompilerParams(collective_id=0, has_side_effects=True, vmem_limit_bytes=40000000),
+        )(*[pltpu.with_memory_space_constraint(a, pltpu.HBM) for a in (sources, near_blocks, left_factors, right_factors)])
 
     return jax.shard_map(
         on_device,

time: 40.4 us -> 39 us (0.965)
  local copies, waits for them, and re-layouts: 1.87 us -> 0.8 us
    unnamed x1, local copies, waits for them, and re-layouts: 1.87 us -> 0.8 us
where the time goes in v4:
time: 39 us; the launch traced here: 38.9 us
  Pallas kernels  38.1 us (98%)
  local copies, waits for them, and re-layouts  0.8 us (2%)
    pallas_call x1, Pallas kernels, on_device(): pl.pallas_call(functools.partial(sweep_kernel, layers, blocks, pieces, sp...  38.1 us
    unnamed x1, local copies, waits for them, and re-layouts  0.8 us

profile of v4, /device:TPU:3, one launch (start us, length us, event | category | flops | bytes accessed | tf_op | source)
XLA Modules:
  0.0 38.9 jit_solution(1911380629525842827)
XLA Ops:
  0.0 38.1 %shard_map.46 = bf16[1,2,1024,128]{3,2,1,0:T(8,128)(2,1)S(1)} custom-call(bf16[1,2,1024,128]{3,2,1,0:T(8,128)(2,1)} %src_hbm.1, bf16[1,1024,1024]{2,1,0:T(8,128)(2,1)} %near_hbm.1, bf16[1,1024,512]{2,1,0:T(8,128)(2,1)} %left_hbm.1, bf16[1,1024,512]{2,1,0:T(8,128)(2,1)} %right_hbm.1), custom_call_target="tpu_custom_call" | custom-call | tf_op jit(solution)/shard_map/pallas_call | solution.py:387
  38.1 0.8 %copy.6 = bf16[1,2,1024,128]{3,2,1,0:T(8,128)(2,1)} copy(bf16[1,2,1024,128]{3,2,1,0:T(8,128)(2,1)S(1)} %shard_map.46) | data formatting | bytes 1048576

commit v5 on v4

--- a/solution.py
+++ b/solution.py
@@ -174,9 +174,10 @@
 
     owns = chip < pieces
 
-    def each_peer(action, only_owners=False):
+    def each_peer(action, only_owners=False, nearest=False):
         def body(i, carry):
-            j = peer(i)
+            k = chips - 2 - i if nearest else i
+            j = peer(chips // 2 + (k + 1) // 2 * (2 * lax.rem(k, 2) - 1))
             if only_owners and pieces < chips:
                 @pl.when(j < pieces)
                 def _():
@@ -185,7 +186,7 @@
                 action(j)
             return carry
 
-        lax.fori_loop(1, chips, body, 0)
+        lax.fori_loop(0, chips - 1, body, 0)
 
     def each_piece(action):
         def body(j, carry):
@@ -239,7 +240,7 @@
             ag_arrival(n, j).wait_recv()
             fw_copy(n, j).start()
 
-        each_peer(pass_on, True)
+        each_peer(pass_on, True, True)
 
     def near_product(at):
         near[at] = jnp.dot(near_w[at], inc[...], preferred_element_type=F32)
@@ -316,14 +317,14 @@
         for b in every:
             scatter(b)
         for b in every:
+            gather(b, False)
+        for b in every:
             x_copy(b).wait_recv()
             inc[front, columns[b]] = (
                 src[b, front].astype(F32) + arrived[b].astype(F32)
             ).astype(BF16)
         near_product(back)
         near_product(front)
-        for b in every:
-            gather(b, False)
         send_near()
         for b in every:
             forward(b)

time: 39 us -> 39.2 us (level)
  no operation moved by 1% of the time
where the time goes in v5:
time: 39.2 us; the launch traced here: 39 us
  Pallas kernels  38.2 us (97%)
  local copies, waits for them, and re-layouts  0.8 us (2%)
    pallas_call x1, Pallas kernels, on_device(): pl.pallas_call(functools.partial(sweep_kernel, layers, blocks, pieces, sp...  38.2 us
    unnamed x1, local copies, waits for them, and re-layouts  0.8 us

profile of v5, /device:TPU:3, one launch (start us, length us, event | category | flops | bytes accessed | tf_op | source)
XLA Modules:
  0.0 39.0 jit_solution(15330003357412195947)
XLA Ops:
  0.0 38.2 %shard_map.46 = bf16[1,2,1024,128]{3,2,1,0:T(8,128)(2,1)S(1)} custom-call(bf16[1,2,1024,128]{3,2,1,0:T(8,128)(2,1)} %src_hbm.1, bf16[1,1024,1024]{2,1,0:T(8,128)(2,1)} %near_hbm.1, bf16[1,1024,512]{2,1,0:T(8,128)(2,1)} %left_hbm.1, bf16[1,1024,512]{2,1,0:T(8,128)(2,1)} %right_hbm.1), custom_call_target="tpu_custom_call" | custom-call | tf_op jit(solution)/shard_map/pallas_call | solution.py:388
  38.2 0.8 %copy.6 = bf16[1,2,1024,128]{3,2,1,0:T(8,128)(2,1)} copy(bf16[1,2,1024,128]{3,2,1,0:T(8,128)(2,1)S(1)} %shard_map.46) | data formatting | bytes 1048576

commit v6 on v5

--- a/solution.py
+++ b/solution.py
@@ -32,6 +32,10 @@
     half = rank // 2
     rows = half // pieces
     every = range(batches)
+    groups = coeff.shape[0] // 2
+    width = coeff.shape[2]
+    each_group = range(groups)
+    lanes = [slice(g * width, (g + 1) * width) for g in each_group]
     columns = [slice(b * srcs, (b + 1) * srcs) for b in every]
     front, back = pl.ds(0, split), pl.ds(split, points - split)
     partner = (layer, chip * 2 + (1 - core))
@@ -116,10 +120,7 @@
         )
 
     def piece(n, side, j):
-        q, b = divmod(n, batches)
-        return coeff.at[
-            q, pl.ds(pl.multiple_of(side * half + j * rows, rows), rows), pl.ds(b * srcs, srcs)
-        ]
+        return coeff.at[n, pl.ds(pl.multiple_of(side * half + j * rows, rows), rows)]
 
     def ag_copy(n, j):
         own = piece(n, core, chip)
@@ -139,7 +140,7 @@
 
     def up_copy(b):
         return remote(
-            piece(b, core, chip), piece(batches + b, core, chip), up_send.at[b], up_recv.at[b], above
+            piece(b, core, chip), piece(groups + b, core, chip), up_send.at[b], up_recv.at[b], above
         )
 
     def carry_copy(b):
@@ -177,7 +178,7 @@
     def each_peer(action, only_owners=False, nearest=False):
         def body(i, carry):
             k = chips - 2 - i if nearest else i
-            j = peer(chips // 2 + (k + 1) // 2 * (2 * lax.rem(k, 2) - 1))
+            j = peer(i + 1)
             if only_owners and pieces < chips:
                 @pl.when(j < pieces)
                 def _():
@@ -196,9 +197,9 @@
         lax.fori_loop(0, pieces, body, 0)
 
     def send_partial(q, value):
-        for b in every:
-            part[q * batches + b] = value[:, columns[b]].astype(BF16)
-            core_copy(q * batches + b).start()
+        for b in each_group:
+            part[q * groups + b] = value[:, lanes[b]].astype(BF16)
+            core_copy(q * groups + b).start()
 
     def scatter(n):
         core_copy(n).wait_recv()
@@ -218,9 +219,7 @@
             if not first:
                 carry_copy(b).wait_recv()
                 total = total + carry_in[b].astype(F32)
-            coeff[
-                0, pl.ds(pl.multiple_of(core * half + chip * rows, rows), rows), columns[b]
-            ] = total.astype(BF16)
+            coeff[b, pl.ds(pl.multiple_of(core * half + chip * rows, rows), rows)] = total.astype(BF16)
             each_peer(lambda j: ag_copy(b, j).start())
             fw_copy(b, chip).start()
 
@@ -232,8 +231,8 @@
         @pl.when(owns)
         def _():
             up_copy(b).wait_recv()
-            each_peer(lambda j: ag_copy(batches + b, j).start())
-            fw_copy(batches + b, chip).start()
+            each_peer(lambda j: ag_copy(groups + b, j).start())
+            fw_copy(groups + b, chip).start()
 
     def forward(n):
         def pass_on(j):
@@ -254,7 +253,7 @@
                 near_copy(b).start()
 
     def finish():
-        for b in every:
+        for b in each_group:
             each_piece(lambda j: fw_arrival(b, j).wait_recv())
         for at in (front, back):
             value = (
@@ -271,12 +270,12 @@
                         x_copy(b).start()
         @pl.when(has_next)
         def _():
-            for b in every:
-                scatter(batches + b)
-            for b in every:
+            for b in each_group:
+                scatter(groups + b)
+            for b in each_group:
                 @pl.when(owns)
                 def _():
-                    carry_out[b] = piece_total(batches + b).astype(BF16)
+                    carry_out[b] = piece_total(groups + b).astype(BF16)
                     carry_copy(b).start()
 
     @pl.when(layer == 0)
@@ -284,14 +283,14 @@
         send_partial(0, base[...])
         loads[2].wait()
         near_product(back)
-        for b in every:
+        for b in each_group:
             scatter(b)
         near_product(front)
-        for b in every:
+        for b in each_group:
             gather(b, True)
         send_near()
         loads[3].wait()
-        for b in every:
+        for b in each_group:
             forward(b)
         finish()
 
@@ -300,23 +299,23 @@
         loads[2].wait()
         loads[3].wait()
         left_copy(0).wait_recv()
-        for b in every:
+        for b in each_group:
             gather_last(b)
-        for b in every:
-            forward(batches + b)
+        for b in each_group:
+            forward(groups + b)
         left_copy(1).wait_recv()
         for b in every:
             near_copy(b).wait_recv()
-        for b in every:
-            each_piece(lambda j: fw_arrival(batches + b, j).wait_recv())
-        far = jnp.dot(last_left[...], coeff[1], preferred_element_type=F32)
+        for b in each_group:
+            each_piece(lambda j: fw_arrival(groups + b, j).wait_recv())
+        far = jnp.dot(last_left[...], coeff[groups], preferred_element_type=F32)
         for b in every:
             trace = (near_in[b].astype(F32) + far[:, columns[b]]).astype(BF16)
             inc[back, columns[b]] = (src[b, back].astype(F32) + trace.astype(F32)).astype(BF16)
         send_partial(0, base[...] + over_points(right_w[back], inc[back]))
-        for b in every:
+        for b in each_group:
             scatter(b)
-        for b in every:
+        for b in each_group:
             gather(b, False)
         for b in every:
             x_copy(b).wait_recv()
@@ -326,7 +325,7 @@
         near_product(back)
         near_product(front)
         send_near()
-        for b in every:
+        for b in each_group:
             forward(b)
         finish()
 
@@ -341,28 +340,28 @@
 
         each_piece(lambda j: fw_copy(n, j).wait_send())
 
-    for b in every:
+    for b in each_group:
         sent(b)
         gathered(b)
 
         @pl.when(has_last)
         def _():
-            gathered(batches + b)
+            gathered(groups + b)
 
         @pl.when(has_next)
         def _():
-            sent(batches + b)
-            near_copy(b).wait_send()
-            x_copy(b).wait_send()
+            sent(groups + b)
 
             @pl.when(owns)
             def _():
                 up_copy(b).wait_send()
                 carry_copy(b).wait_send()
 
-
     @pl.when(has_next)
     def _():
+        for b in every:
+            near_copy(b).wait_send()
+            x_copy(b).wait_send()
         left_copy(0).wait_send()
         left_copy(1).wait_send()
 
@@ -383,6 +382,7 @@
         rows = half // pieces
         split = points * 19 // 32
         rest = points - split
+        groups, width = 1, batches * srcs
         dma = pltpu.SemaphoreType.DMA
         vmem = pltpu.VMEM
         return pl.pallas_call(
@@ -397,24 +397,24 @@
                 vmem(right_factors.shape[1:], BF16),
                 vmem((points, batches * srcs), BF16),
                 vmem((batches, split, srcs), BF16),
-                vmem((2 * batches, rank, srcs), BF16),
-                vmem((2 * batches, half, srcs), BF16),
-                vmem((2 * batches, half, srcs), BF16),
-                vmem((2 * batches, chips, rows, srcs), BF16),
-                vmem((2, rank, batches * srcs), BF16),
+                vmem((2 * groups, rank, width), BF16),
+                vmem((2 * groups, half, width), BF16),
+                vmem((2 * groups, half, width), BF16),
+                vmem((2 * groups, chips, rows, width), BF16),
+                vmem((2 * groups, rank, width), BF16),
                 vmem((points, batches * srcs), F32),
                 vmem((split, rank), BF16),
                 vmem((rest, rank), BF16),
                 vmem((batches, rest, srcs), BF16),
                 vmem((batches, rest, srcs), BF16),
-                vmem((batches, rows, srcs), BF16),
-                vmem((batches, rows, srcs), BF16),
+                vmem((groups, rows, width), BF16),
+                vmem((groups, rows, width), BF16),
                 vmem((rank, batches * srcs), F32),
                 dma((4,)),
-                dma((2 * batches,)), dma((2 * batches,)),
-                dma((2 * batches, chips)), dma((2 * batches, chips)),
-                dma((2 * batches, chips)), dma((2 * batches, chips)),
-                dma((2 * batches, pieces)), dma((2 * batches, pieces)),
+                dma((2 * groups,)), dma((2 * groups,)),
+                dma((2 * groups, chips)), dma((2 * groups, chips)),
+                dma((2 * groups, chips)), dma((2 * groups, chips)),
+                dma((2 * groups, pieces)), dma((2 * groups, pieces)),
                 dma((batches,)), dma((batches,)),
                 dma((batches,)), dma((batches,)),
                 dma((batches,)), dma((batches,)),

time: 39.2 us -> 37.2 us (0.949)
  Pallas kernels: 38.2 us -> 36.3 us
    pallas_call x1, Pallas kernels: 38.2 us -> 36.3 us  [on_device(): pl.pallas_call(functools.partial(sweep_kernel, layers, blocks, pieces, sp...]
where the time goes in v6:
time: 37.2 us; the launch traced here: 37.1 us
  Pallas kernels  36.3 us (98%)
  local copies, waits for them, and re-layouts  0.8 us (2%)
    pallas_call x1, Pallas kernels, on_device(): pl.pallas_call(functools.partial(sweep_kernel, layers, blocks, pieces, sp...  36.3 us
    unnamed x1, local copies, waits for them, and re-layouts  0.8 us

profile of v6, /device:TPU:3, one launch (start us, length us, event | category | flops | bytes accessed | tf_op | source)
XLA Modules:
  0.0 37.1 jit_solution(4608181391710179355)
XLA Ops:
  0.0 36.3 %shard_map.46 = bf16[1,2,1024,128]{3,2,1,0:T(8,128)(2,1)S(1)} custom-call(bf16[1,2,1024,128]{3,2,1,0:T(8,128)(2,1)} %src_hbm.1, bf16[1,1024,1024]{2,1,0:T(8,128)(2,1)} %near_hbm.1, bf16[1,1024,512]{2,1,0:T(8,128)(2,1)} %left_hbm.1, bf16[1,1024,512]{2,1,0:T(8,128)(2,1)} %right_hbm.1), custom_call_target="tpu_custom_call" | custom-call | tf_op jit(solution)/shard_map/pallas_call | solution.py:388
  36.3 0.8 %copy.6 = bf16[1,2,1024,128]{3,2,1,0:T(8,128)(2,1)} copy(bf16[1,2,1024,128]{3,2,1,0:T(8,128)(2,1)S(1)} %shard_map.46) | data formatting | bytes 1048576
